TPU v7x, 32 devices: a whole 2x2x4 slice. The times are simulated.
32 devices in a mesh: groups: 2 (over y), fsdp: 4 (over z), expert: 4 (over x, core).
Axes of the slice: x: 2, y: 2, z: 4, core: 2. Of those that a mesh axis runs over, the one named last changes fastest.
Arguments:
- queries: bfloat16 [512, 2048], P(('groups', 'fsdp'), 'expert'), parts along dimension 0, may hold values from -14 to 14
- keys: bfloat16 [8, 2048, 512], P(('groups', 'fsdp'), None, 'expert'), parts along dimension 0, may hold values from -14 to 14
- values: bfloat16 [8, 2048, 512], P(('groups', 'fsdp'), None, 'expert'), parts along dimension 0, may hold values from -4 to 4
- out_weight: bfloat16 [2048, 4096], P('expert', 'fsdp'), may hold values from -0.5 to 0.5
- residual: bfloat16 [512, 4096], P(('groups', 'fsdp')), parts along dimension 0, may hold values from -3 to 3
- norm_gain: float32 [4096], replicated, may hold values from 0.5 to 1.5
- route_ids: int32 [512, 2], P(('groups', 'fsdp')), parts along dimension 0, may hold values from 0 to 7, as said below
- route_slots: int32 [512, 2], P(('groups', 'fsdp')), parts along dimension 0, may hold values from 0 to 23, as said below
- route_weights: int32 [512, 2], P(('groups', 'fsdp')), parts along dimension 0, may hold values from 1 to 65535, as said below
- w_gate: bfloat16 [8, 4096, 7168], P('expert', None, 'fsdp'), may hold values from -0.09375 to 0.09375
- w_up: bfloat16 [8, 4096, 7168], P('expert', None, 'fsdp'), may hold values from -0.09375 to 0.09375
- w_down: bfloat16 [8, 7168, 4096], P('expert', 'fsdp'), may hold values from -0.0625 to 0.0625
Outputs:
- layer_out: bfloat16 [512, 4096], P(('groups', 'fsdp'), 'expert'), parts along dimension 0
There are 2 independent parts, one for each index of `groups`. A program takes and returns all parts, laid end to end along the dimension named above; an argument that names none is the same for every part. Nothing has to cross between parts.
Inputs may be any that keep to these rules, and one draw needn't show every extreme that they name: `route_ids`: each row names two different experts. Among the rows of one block, no expert is named more than 24 times and no group of experts 2 g and 2 g + 1 more than 36 times; one expert, the same for all blocks, is named exactly 24 times in every block and its group exactly 36 times; every expert is named in every block. `route_slots`: within one block, the routes to one expert hold the slots 0 to their count - 1, each once. `route_weights`: the two entries of a row sum to 65536.
All inputs are finite; a program needn't handle non-finite values.
Results may differ from a plain program's by a relative error of at most 0.02.
Values may be sent and summed in bfloat16 or wider, within the bound.
A program may use at most 192 MiB of HBM per device.

v0:
```python
import functools

import jax
import jax.numpy as jnp
from jax import lax
from jax.experimental import pallas as pl
from jax.experimental.pallas import tpu as pltpu
from jax.sharding import PartitionSpec as P

HEAD_DIM = 128
CAP = 24
EPS = 1e-05
MESH = pl.DeviceIdType.MESH
F32 = jnp.float32
BF16 = jnp.bfloat16


def loop(low, high, body):
    if high - low <= 8:
        for i in range(low, high):
            body(i)
    else:
        lax.fori_loop(low, high, lambda i, c: (body(i), c)[1], 0)


def kernel(
    F, G,
    q_ref, k_ref, v_ref, ow_ref, res_ref, gain_ref, rt_ref, wg_ref, wu_ref, wd_ref,
    out_ref,
    heads, routes, res_in, part, rs_in, h_all, oh, lhs, ssq, acc, hid, ybuf,
    cbuf, a_in, b_in, c_in, wslot, dslot,
    hs_s, hs_r, rt_s, rt_r, re_s, re_r, rs_s, rs_r, hz_s, hz_r, hx_s, hx_r, hc_s, hc_r,
    a_s, a_r, b_s, b_r, c_s, c_r, w_sem, d_sem,
):
    f = lax.axis_index("fsdp")
    g = lax.axis_index("expert")
    FG = F // G
    Q = q_ref.shape[0]
    ctx = k_ref.shape[0]
    C = ow_ref.shape[1]
    D = wg_ref.shape[1]
    R = CAP * F
    C2 = D // G
    n_heads = q_ref.shape[1] // HEAD_DIM

    def xor(a, m):
        low = a % 2
        high = a // 2
        if m & 1:
            low = 1 - low
        if m & 2:
            high = 1 - high
        return high * 2 + low

    def copy(src, dst, s, r, **dev):
        return pltpu.make_async_remote_copy(
            src_ref=src, dst_ref=dst, send_sem=s, recv_sem=r,
            device_id=dev, device_id_type=MESH,
        )

    def w_copies(k):
        col = lax.rem(f + k, F)
        rows = pl.ds(pl.multiple_of(col * C, C), C)
        two = k % 2
        out = []
        for e in range(2):
            for t, ref in enumerate((wg_ref, wu_ref)):
                out.append(pltpu.make_async_copy(
                    ref.at[e, rows, :], wslot.at[two, 2 * e + t], w_sem.at[two, 2 * e + t]))
        return out

    masks = (3, 2, 1, 0)

    def d_copies(i):
        block = xor(g, masks[i]) if masks[i] else g
        cols = pl.ds(pl.multiple_of(block * C2, C2), C2)
        return [
            pltpu.make_async_copy(wd_ref.at[e, :, cols], dslot.at[i % 2, e], d_sem.at[i % 2, e])
            for e in range(2)
        ]

    for k in range(min(2, F)):
        for c in w_copies(k):
            c.start()
    for i in range(2):
        for c in d_copies(i):
            c.start()

    barrier = pltpu.get_barrier_semaphore()

    def greet_f(i):
        pl.semaphore_signal(barrier, inc=1, device_id={"fsdp": lax.rem(f + i, F)}, device_id_type=MESH)

    loop(1, F, greet_f)
    for i in range(1, G):
        pl.semaphore_signal(
            barrier, inc=1, device_id={"expert": lax.rem(g + i, G)}, device_id_type=MESH)
    pl.semaphore_wait(barrier, F - 1 + G - 1)

    def rt_copy(i):
        return copy(rt_ref, routes.at[f], rt_s.at[i], rt_r.at[f], fsdp=lax.rem(f + i, F))

    def rt_got(i):
        p = lax.rem(f + i, F)
        return copy(rt_ref, routes.at[p], rt_s.at[i], rt_r.at[p], fsdp=p)

    def cols_of(p):
        return pl.ds(pl.multiple_of(p * C, C), C)

    own_part = (f // FG) == g
    mine = f % FG

    def re_copy(i):
        p = lax.rem(f + i, F)
        return copy(res_ref.at[:, cols_of(p)], res_in.at[mine], re_s.at[i], re_r.at[mine], fsdp=p)

    loop(1, F, lambda i: rt_copy(i).start())

    @pl.when(own_part)
    def _():
        loop(1, F, lambda i: re_copy(i).start())
        res_in[mine] = res_ref[:, cols_of(f)]

    routes[f] = rt_ref[...]

    key_pos = lax.broadcasted_iota(jnp.int32, (Q, ctx), 1)
    query_pos = ctx - Q + lax.broadcasted_iota(jnp.int32, (Q, ctx), 0)
    allowed = key_pos <= query_pos
    n_kv = k_ref.shape[1] // HEAD_DIM
    for h in range(n_heads):
        kv = h // (n_heads // n_kv)
        qh = q_ref[:, h * HEAD_DIM:(h + 1) * HEAD_DIM]
        kh = k_ref[:, kv * HEAD_DIM:(kv + 1) * HEAD_DIM]
        vh = v_ref[:, kv * HEAD_DIM:(kv + 1) * HEAD_DIM]
        s = lax.dot_general(qh, kh, (((1,), (1,)), ((), ())), preferred_element_type=F32)
        s = jnp.where(allowed, s * HEAD_DIM ** (-0.5), -1e30)
        top = jnp.max(s, axis=1, keepdims=True)
        w = jnp.exp(s - top)
        total = jnp.sum(w, axis=1, keepdims=True)
        p = (w / total).astype(BF16)
        o = jnp.dot(p, vh, preferred_element_type=F32)
        heads[f, :, h * HEAD_DIM:(h + 1) * HEAD_DIM] = o.astype(BF16)

    def hs_copy(i):
        return copy(heads.at[f], heads.at[f], hs_s.at[i], hs_r.at[f], fsdp=lax.rem(f + i, F))

    def hs_got(i):
        p = lax.rem(f + i, F)
        return copy(heads.at[p], heads.at[p], hs_s.at[i], hs_r.at[p], fsdp=p)

    loop(1, F, lambda i: hs_copy(i).start())

    loop(1, F, lambda i: rt_got(i).wait_recv())

    def tables(s):
        r = routes[s]
        slot_row = lax.broadcasted_iota(jnp.int32, (2 * CAP, Q), 0)
        table = jnp.zeros((2 * CAP, Q), F32)
        weight = jnp.zeros((2 * CAP, Q), F32)
        for t in range(2):
            within = r[t:t + 1, :Q] - 2 * g
            inside = (within >= 0) & (within < 2)
            row = jnp.where(inside, r[2 + t:3 + t, :Q] + CAP * within, -1)
            hit = (row == slot_row).astype(F32)
            table = table + hit
            weight = weight + hit * (r[4 + t:5 + t, :Q].astype(F32) / 65536.0)
        oh[s, :, :Q] = table
        oh[s, :, Q:] = jnp.broadcast_to(jnp.sum(weight, axis=1, keepdims=True), (2 * CAP, 128 - Q))

    loop(0, F, tables)
    ssq[...] = jnp.zeros_like(ssq)
    loop(1, F, lambda i: hs_got(i).wait_recv())

    def rs_copy(i):
        j = lax.rem(g + i, G)
        return copy(part.at[i - 1], rs_in.at[i - 1], rs_s.at[i], rs_r.at[i], expert=j)

    def rs_got(i):
        j = lax.rem(g + i, G)
        return copy(part.at[i - 1], rs_in.at[i - 1], rs_s.at[i], rs_r.at[i], expert=j)

    def project(j):
        rows = heads[pl.ds(j * FG, FG)].reshape(FG * Q, n_heads * HEAD_DIM)
        return jnp.dot(rows, ow_ref[...], preferred_element_type=F32).reshape(FG, Q, C)

    for i in (2, 3, 1):
        j = lax.rem(g + i, G)
        part[i - 1] = project(j).astype(BF16)
        rs_copy(i).start()
    attn = project(g)

    def re_got(i):
        p = g * FG + i
        return copy(res_in.at[i], res_in.at[i], re_s.at[0], re_r.at[i], fsdp=p)

    def take_res(i):
        @pl.when(g * FG + i != f)
        def _():
            re_got(i).wait_recv()

    loop(0, FG, take_res)
    for i in (1, 3, 2):
        rs_got(i).wait_recv()
        attn = attn + rs_in[i - 1].astype(F32)
    h_all[f, pl.ds(g * FG, FG)] = (res_in[...].astype(F32) + attn).astype(BF16)

    def chunk(p, e):
        return h_all.at[p, pl.ds(e * FG, FG)]

    far, near, both = xor(g, 2), xor(g, 1), xor(g, 3)

    def hz_copy(i):
        return copy(chunk(f, g), chunk(f, g), hz_s.at[i], hz_r.at[f], fsdp=lax.rem(f + i, F))

    def hz_got(i):
        p = lax.rem(f + i, F)
        return copy(chunk(p, g), chunk(p, g), hz_s.at[i], hz_r.at[p], fsdp=p)

    def hx_copy(k):
        p = lax.rem(f + k, F)
        return copy(chunk(p, g), chunk(p, g), hx_s.at[k], hx_r.at[k], expert=far)

    def hx_got(k):
        p = lax.rem(f + k, F)
        return copy(chunk(p, far), chunk(p, far), hx_s.at[k], hx_r.at[k], expert=far)

    def hc_copy(k, t):
        p = lax.rem(f + k, F)
        c = chunk(p, (g, far)[t])
        return copy(c, c, hc_s.at[k, t], hc_r.at[k, t], expert=near)

    def hc_got(k, t):
        p = lax.rem(f + k, F)
        c = chunk(p, (near, both)[t])
        return copy(c, c, hc_s.at[k, t], hc_r.at[k, t], expert=near)

    hx_copy(0).start()
    loop(1, F, lambda i: hz_copy(F - i).start())
    hc_copy(0, 0).start()

    def step(k):
        def ahead(n):
            hz_got(n).wait_recv()
            hx_copy(n).start()
            hc_copy(n, 0).start()

        if isinstance(k, int):
            if k + 1 < F:
                ahead(k + 1)
        else:
            pl.when(k + 1 < F)(lambda: ahead(k + 1))
        p = lax.rem(f + k, F)
        hx_got(k).wait_recv()
        hc_copy(k, 1).start()
        hc_got(k, 0).wait_recv()
        hc_got(k, 1).wait_recv()
        gain = gain_ref[p]

        def dispatch(s):
            rows = jnp.dot(oh[s, :, :Q].astype(BF16), h_all[p, s], preferred_element_type=F32)
            at = s * CAP if isinstance(s, int) else pl.multiple_of(s * CAP, 8)
            square = jnp.sum(rows * rows, axis=1, keepdims=True)
            rows = rows * gain
            for e in range(2):
                lhs[e, pl.ds(at, CAP), :] = rows[e * CAP:(e + 1) * CAP]
                ssq[e, pl.ds(at, CAP), :] += jnp.broadcast_to(square[e * CAP:(e + 1) * CAP], (CAP, 128))

        loop(0, F, dispatch)
        two = k % 2
        copies = w_copies(k)
        for e in range(2):
            x = lhs[e].astype(BF16)
            for t in range(2):
                copies[2 * e + t].wait()
                y = jnp.dot(x, wslot[two, 2 * e + t], preferred_element_type=F32)
                if isinstance(k, int) and k == 0:
                    acc[e, t] = y
                else:
                    acc[e, t] += y

        def refill():
            for c in w_copies(k + 2):
                c.start()

        if isinstance(k, int):
            if k + 2 < F:
                refill()
        else:
            pl.when(k + 2 < F)(refill)

    if F > 8:
        acc[...] = jnp.zeros_like(acc)
    loop(0, F, step)

    for e in range(2):
        scale = lax.rsqrt(ssq[e][:, :1] / D + EPS)
        gate = acc[e, 0] * scale
        up = acc[e, 1] * scale
        hid[e] = (gate / (1.0 + jnp.exp(-gate)) * up).astype(BF16)

    def a_copy(t):
        return copy(cbuf.at[0], a_in.at[t], a_s.at[t], a_r.at[t], expert=near)

    place = (0, 1, 0, 2)

    def b_copy(s):
        return copy(cbuf.at[1, s], b_in.at[s], b_s.at[s], b_r.at[s], expert=far)

    for i in range(4):
        copies = d_copies(i)
        for e in range(2):
            copies[e].wait()
            ybuf[e] = jnp.dot(hid[e], dslot[i % 2, e], preferred_element_type=F32)
        if i + 2 < 4:
            for c in d_copies(i + 2):
                c.start()

        if i in (1, 3):
            a_copy(i // 2).wait_recv()
        if i == 2:
            a_copy(0).wait_send()

        def combine(s):
            at = s * CAP if isinstance(s, int) else pl.multiple_of(s * CAP, 8)
            ys = jnp.concatenate([ybuf[0, pl.ds(at, CAP), :], ybuf[1, pl.ds(at, CAP), :]], axis=0)
            ys = (ys * oh[s, :, Q:Q + 1]).astype(BF16)
            c = lax.dot_general(
                oh[s, :, :Q].astype(BF16), ys, (((0,), (0,)), ((), ())), preferred_element_type=F32)
            if i in (1, 3):
                c = c + a_in[i // 2, s].astype(F32)
            cbuf[place[i], s] = c.astype(BF16)

        def send_far(n):
            s = lax.rem(f + 1 + n, F)
            combine(s)
            b_copy(s).start()

        loop(0, F, send_far if i == 1 else combine)
        if i in (0, 2):
            a_copy(i // 2).start()

    def c_copy(s):
        return copy(cbuf.at[2, s], c_in.at[f], c_s.at[s], c_r.at[f], fsdp=s)

    def c_got(i):
        p = lax.rem(f + i, F)
        return copy(c_in.at[p], c_in.at[p], c_s.at[p], c_r.at[p], fsdp=p)

    def send_seq(n):
        s = lax.rem(f + 1 + n, F)
        b_copy(s).wait_recv()
        cbuf[2, s] = (cbuf[2, s].astype(F32) + b_in[s].astype(F32)).astype(BF16)
        c_copy(s).start()

    loop(0, F - 1, send_seq)
    b_copy(f).wait_recv()
    total = cbuf[2, f].astype(F32) + b_in[f].astype(F32)
    ybuf[0, 0:Q, :] = total

    def add_seq(i):
        c_got(i).wait_recv()
        ybuf[0, 0:Q, :] += c_in[lax.rem(f + i, F)].astype(F32)

    loop(1, F, add_seq)
    for i in range(FG):
        state = h_all[g * FG + i, f].astype(F32)
        out_ref[:, i * C:(i + 1) * C] = (state + ybuf[0, 0:Q, i * C:(i + 1) * C]).astype(BF16)

    def drain(i):
        rt_copy(i).wait_send()
        hs_copy(i).wait_send()
        hz_copy(i).wait_send()
        c_copy(lax.rem(f + i, F)).wait_send()

    loop(1, F, drain)

    @pl.when(own_part)
    def _():
        loop(1, F, lambda i: re_copy(i).wait_send())

    for i in range(1, G):
        rs_copy(i).wait_send()

    def drain_all(k):
        hx_copy(k).wait_send()
        hc_copy(k, 0).wait_send()
        hc_copy(k, 1).wait_send()
        b_copy(k).wait_send()

    loop(0, F, drain_all)
    a_copy(1).wait_send()


def layer(F, G, queries, keys, values, out_weight, residual, norm_gain,
          route_ids, route_slots, route_weights, w_gate, w_up, w_down):
    Q = queries.shape[0]
    D = residual.shape[1]
    C = out_weight.shape[1]
    H = w_gate.shape[2]
    R = CAP * F
    FG = F // G
    C2 = D // G
    table = jnp.concatenate([route_ids.T, route_slots.T, route_weights.T], axis=0)
    table = jnp.pad(table, ((0, 2), (0, 128 - Q)))
    gain = norm_gain.reshape(F, 1, C)
    vm = pl.BlockSpec(memory_space=pltpu.VMEM)
    hbm = pl.BlockSpec(memory_space=pltpu.HBM)
    dma = pltpu.SemaphoreType.DMA
    return pl.pallas_call(
        functools.partial(kernel, F, G),
        out_shape=jax.ShapeDtypeStruct((Q, C2), BF16),
        in_specs=[vm] * 7 + [hbm] * 3,
        out_specs=vm,
        scratch_shapes=[
            pltpu.VMEM((F, Q, queries.shape[1]), BF16),
            pltpu.VMEM((F, 8, 128), jnp.int32),
            pltpu.VMEM((FG, Q, C), BF16),
            pltpu.VMEM((G - 1, FG, Q, C), BF16),
            pltpu.VMEM((G - 1, FG, Q, C), BF16),
            pltpu.VMEM((F, F, Q, C), BF16),
            pltpu.VMEM((F, 2 * CAP, 128), F32),
            pltpu.VMEM((2, R, C), F32),
            pltpu.VMEM((2, R, 128), F32),
            pltpu.VMEM((2, 2, R, H), F32),
            pltpu.VMEM((2, R, H), BF16),
            pltpu.VMEM((2, R, C2), F32),
            pltpu.VMEM((3, F, Q, C2), BF16),
            pltpu.VMEM((2, F, Q, C2), BF16),
            pltpu.VMEM((F, Q, C2), BF16),
            pltpu.VMEM((F, Q, C2), BF16),
            pltpu.VMEM((2, 4, C, H), BF16),
            pltpu.VMEM((2, 2, H, C2), BF16),
            dma((F,)), dma((F,)), dma((F,)), dma((F,)), dma((F,)), dma((FG,)),
            dma((G,)), dma((G,)), dma((F,)), dma((F,)), dma((F,)), dma((F,)),
            dma((F, 2)), dma((F, 2)), dma((2,)), dma((2,)), dma((F,)), dma((F,)),
            dma((F,)), dma((F,)), dma((2, 4)), dma((2, 2)),
        ],
        compiler_params=pltpu.CompilerParams(
            collective_id=0, has_side_effects=True, vmem_limit_bytes=67043328),
    )(queries, keys[0], values[0], out_weight, residual, gain, table, w_gate, w_up, w_down)


def solution(mesh):
    F, G = mesh.shape["fsdp"], mesh.shape["expert"]
    rows = P(("groups", "fsdp"), None)
    in_specs = (
        P(("groups", "fsdp"), "expert"),
        P(("groups", "fsdp"), None, "expert"),
        P(("groups", "fsdp"), None, "expert"),
        P("expert", "fsdp"),
        rows, P(), rows, rows, rows,
        P("expert", None, "fsdp"),
        P("expert", None, "fsdp"),
        P("expert", "fsdp", None),
    )
    return jax.shard_map(
        functools.partial(layer, F, G), mesh=mesh, in_specs=in_specs,
        out_specs=P(("groups", "fsdp"), "expert"), check_vma=False,
    )
```

profile of v0, /device:TPU:0, one launch (start us, length us, event | category | flops | bytes accessed | tf_op | source)
XLA Modules:
  0.0 77.6 jit_solution(5616269296085837159)
XLA Ops:
  0.0 0.7 pad_add_fusion
  0.7 0.6 pad.4.rt_ref
  1.3 74.7 %shard_map.118 = bf16[64,1024]{1,0:T(8,128)(2,1)} custom-call(bf16[64,512]{1,0:T(8,128)(2,1)} %q_ref.1, bf16[2048,128]{1,0:T(8,128)(2,1)} %bitcast.6, bf16[2048,128]{1,0:T(8,128)(2,1)} %bitcast.7, bf16[512,1024]{1,0:T(8,128)(2,1)} %ow_ref.1, bf16[64,4096]{1,0:T(8,128)(2,1)} %res_ref.1, f32[4,1,1024]{2,1,0:T(1,128)} %bitcast.8, s32[8,128]{1,0:T(8,128)} %pad.4.rt_ref, ...), custom_call_target="tpu_custom_call" | custom-call | tf_op jit(solution)/shard_map/pallas_call | solution.py:409
  76.1 1.6 %copy.14 = bf16[64,1024]{1,0:T(8,128)(2,1)} copy(bf16[64,1024]{1,0:T(8,128)(2,1)} %shard_map.118) | data formatting | bytes 262144
where the time goes:
time: 77.8 us; the launch traced here: 77.6 us
  Pallas kernels  74.7 us (96%)
  local copies, waits for them, and re-layouts  2.17 us (3%)
    pallas_call x1, Pallas kernels, layer(): pl.pallas_call(functools.partial(kernel, F, G), out_shape=jax.ShapeDtypeS...  74.7 us
    unnamed x1, local copies, waits for them, and re-layouts  1.57 us

commit v1 on v0

v1 whole, which is shorter than its diff:
```python
import functools

import jax
import jax.numpy as jnp
from jax import lax
from jax.experimental import pallas as pl
from jax.experimental.pallas import tpu as pltpu
from jax.sharding import PartitionSpec as P

HEAD_DIM = 128
CAP = 24
EPS = 1e-05
MESH = pl.DeviceIdType.MESH
F32 = jnp.float32
BF16 = jnp.bfloat16
HALVES = 2
D_SLOTS = 4


def loop(low, high, body):
    if high - low <= 8:
        for i in range(low, high):
            body(i)
    else:
        lax.fori_loop(low, high, lambda i, c: (body(i), c)[1], 0)


def when(cond, body):
    if isinstance(cond, bool):
        if cond:
            body()
    else:
        pl.when(cond)(body)


def kernel(
    F, G,
    q_hbm, k_hbm, v_hbm, ow_hbm, res_hbm, gain_ref, ids_ref, slots_ref, wts_ref, wg_ref, wu_ref, wd_ref,
    out_ref,
    q_ref, k_ref, v_ref, ow_ref, res_ref,
    heads, routes, res_in, part, rs_in, attn_own, h_all, oh, lhs, ssq, acc, hid, ybuf,
    cbuf, a_in, b_in, c_in, wslot, dslot,
    in_sem, hs_s, hs_r, rt_s, rt_r, re_s, re_r, rs_s, rs_r, hz_s, hz_r, hx_s, hx_r, hc_s, hc_r,
    a_s, a_r, b_s, b_r, c_s, c_r, w_sem, d_sem,
):
    f = lax.axis_index("fsdp")
    g = lax.axis_index("expert")
    FG = F // G
    Q = q_ref.shape[0]
    ctx = k_ref.shape[0]
    C = ow_ref.shape[1]
    D = wg_ref.shape[1]
    C2 = D // G
    CH = C2 // HALVES
    n_heads = q_ref.shape[1] // HEAD_DIM

    def flip(a, m, n):
        if isinstance(m, int) and m == 0:
            return a
        out = 0
        bit = 1
        while bit < n:
            low = lax.rem(lax.div(a, bit), 2)
            if isinstance(m, int):
                mine = (m // bit) % 2
                low = 1 - low if mine else low
            else:
                mine = lax.rem(lax.div(m, bit), 2)
                low = low + mine - 2 * low * mine
            out = out + bit * low
            bit *= 2
        return out

    def peer(i):
        if F & (F - 1) == 0:
            return flip(f, i, F)
        return lax.rem(f + i, F)

    def copy(src, dst, s, r, **dev):
        return pltpu.make_async_remote_copy(
            src_ref=src, dst_ref=dst, send_sem=s, recv_sem=r,
            device_id=dev, device_id_type=MESH,
        )

    barrier = pltpu.get_barrier_semaphore()

    def greet_f(i):
        pl.semaphore_signal(barrier, inc=1, device_id={"fsdp": lax.rem(f + i, F)}, device_id_type=MESH)

    loop(1, F, greet_f)
    for i in range(1, G):
        pl.semaphore_signal(
            barrier, inc=1, device_id={"expert": lax.rem(g + i, G)}, device_id_type=MESH)

    loads = [
        pltpu.make_async_copy(src, dst, in_sem.at[i])
        for i, (src, dst) in enumerate((
            (q_hbm, q_ref), (k_hbm, k_ref), (v_hbm, v_ref), (res_hbm, res_ref), (ow_hbm, ow_ref)))
    ]
    for c in loads:
        c.start()

    def w_copies(k):
        col = peer(k)
        rows = pl.ds(pl.multiple_of(col * C, C), C)
        two = k % 2
        out = []
        for e in range(2):
            for t, ref in enumerate((wg_ref, wu_ref)):
                out.append(pltpu.make_async_copy(
                    ref.at[e, rows, :], wslot.at[two, 2 * e + t], w_sem.at[two, 2 * e + t]))
        return out

    masks = (3, 2, 1, 0)

    def d_copies(n):
        block = flip(g, masks[n % 4], G)
        cols = pl.ds(pl.multiple_of(block * C2 + (n // 4) * CH, CH), CH)
        return [
            pltpu.make_async_copy(wd_ref.at[e, :, cols], dslot.at[n % D_SLOTS, e], d_sem.at[n % D_SLOTS, e])
            for e in range(2)
        ]

    routes[f] = jnp.zeros((8, 128), jnp.int32)
    for t, ref in enumerate((ids_ref, slots_ref, wts_ref)):
        routes[f, 2 * t:2 * t + 2, :Q] = ref[...]

    n_kv = k_ref.shape[1] // HEAD_DIM
    per = n_heads // n_kv
    rate = HEAD_DIM ** (-0.5) * 1.4426950408889634
    for c in loads:
        c.wait()
    for k in range(min(2, F)):
        for c in w_copies(k):
            c.start()
    for n in range(D_SLOTS):
        for c in d_copies(n):
            c.start()

    for kv in range(n_kv):
        cols = slice(kv * HEAD_DIM, (kv + 1) * HEAD_DIM)
        qs = jnp.concatenate(
            [q_ref[:, h * HEAD_DIM:(h + 1) * HEAD_DIM] for h in range(kv * per, (kv + 1) * per)], axis=0)
        s = lax.dot_general(qs, k_ref[:, cols], (((1,), (1,)), ((), ())), preferred_element_type=F32)
        tail = 128
        key_pos = ctx - tail + lax.broadcasted_iota(jnp.int32, (per, Q, tail), 2)
        query_pos = ctx - Q + lax.broadcasted_iota(jnp.int32, (per, Q, tail), 1)
        allowed = (key_pos <= query_pos).reshape(per * Q, tail)
        s = jnp.concatenate([s[:, :ctx - tail], jnp.where(allowed, s[:, ctx - tail:], -1e30)], axis=1)
        top = jnp.max(s, axis=1, keepdims=True)
        w = jnp.exp2((s - top) * rate)
        total = jnp.sum(w, axis=1, keepdims=True)
        o = jnp.dot(w.astype(BF16), v_ref[:, cols], preferred_element_type=F32) / total
        for n in range(per):
            h = kv * per + n
            heads[f, :, h * HEAD_DIM:(h + 1) * HEAD_DIM] = o[n * Q:(n + 1) * Q].astype(BF16)

    pl.semaphore_wait(barrier, F - 1 + G - 1)

    def rt_copy(i):
        return copy(routes.at[f], routes.at[f], rt_s.at[i], rt_r.at[f], fsdp=peer(i))

    def rt_got(i):
        p = peer(i)
        return copy(routes.at[p], routes.at[p], rt_s.at[i], rt_r.at[p], fsdp=p)

    def cols_of(p):
        return pl.ds(pl.multiple_of(p * C, C), C)

    own_part = (f // FG) == g
    mine = f % FG

    def re_copy(i):
        p = peer(i)
        return copy(res_ref.at[:, cols_of(p)], res_in.at[mine], re_s.at[i], re_r.at[mine], fsdp=p)

    def hs_copy(i):
        return copy(heads.at[f], heads.at[f], hs_s.at[i], hs_r.at[f], fsdp=peer(i))

    def hs_got(p):
        return copy(heads.at[p], heads.at[p], hs_s.at[0], hs_r.at[p], fsdp=p)

    loop(1, F, lambda i: hs_copy(i).start())
    loop(1, F, lambda i: rt_copy(i).start())

    @pl.when(own_part)
    def _():
        loop(1, F, lambda i: re_copy(i).start())
        res_in[mine] = res_ref[:, cols_of(f)]

    ssq[...] = jnp.zeros_like(ssq)

    def rs_copy(j):
        return copy(part.at[j], rs_in.at[g], rs_s.at[j], rs_r.at[g], expert=j)

    def rs_got(e):
        return copy(part.at[e], rs_in.at[e], rs_s.at[e], rs_r.at[e], expert=e)

    def project(i):
        j = flip(f // FG, i, G)

        def arrive(n):
            p = j * FG + n

            @pl.when(p != f)
            def _():
                hs_got(p).wait_recv()

        loop(0, FG, arrive)
        rows = heads[pl.ds(j * FG, FG)].reshape(FG * Q, n_heads * HEAD_DIM)
        y = jnp.dot(rows, ow_ref[...], preferred_element_type=F32).reshape(FG, Q, C)

        @pl.when(j == g)
        def _():
            attn_own[...] = y

        @pl.when(j != g)
        def _():
            part[j] = y.astype(BF16)
            rs_copy(j).start()

    for i in range(G):
        project(i)

    loop(1, F, lambda i: rt_got(i).wait_recv())

    def tables(s):
        r = routes[s]
        slot_row = lax.broadcasted_iota(jnp.int32, (2 * CAP, Q), 0)
        table = jnp.zeros((2 * CAP, Q), F32)
        weight = jnp.zeros((2 * CAP, Q), F32)
        for t in range(2):
            within = r[t:t + 1, :Q] - 2 * g
            inside = (within >= 0) & (within < 2)
            row = jnp.where(inside, r[2 + t:3 + t, :Q] + CAP * within, -1)
            hit = (row == slot_row).astype(F32)
            table = table + hit
            weight = weight + hit * (r[4 + t:5 + t, :Q].astype(F32) / 65536.0)
        oh[s, :, :Q] = table
        oh[s, :, Q:] = jnp.broadcast_to(jnp.sum(weight, axis=1, keepdims=True), (2 * CAP, 128 - Q))

    loop(0, F, tables)

    far, near, both = flip(g, 2, G), flip(g, 1, G), flip(g, 3, G)

    def re_got(i):
        p = g * FG + i
        return copy(res_in.at[i], res_in.at[i], re_s.at[0], re_r.at[i], fsdp=p)

    def take_res(i):
        @pl.when(g * FG + i != f)
        def _():
            re_got(i).wait_recv()

    attn = attn_own[...]
    for e in (near, far, both):
        rs_got(e).wait_recv()
        attn = attn + rs_in[e].astype(F32)
    loop(0, FG, take_res)
    h_all[f, pl.ds(g * FG, FG)] = (res_in[...].astype(F32) + attn).astype(BF16)

    def chunk(p, e):
        return h_all.at[p, pl.ds(e * FG, FG)]

    def hz_copy(i):
        return copy(chunk(f, g), chunk(f, g), hz_s.at[i], hz_r.at[f], fsdp=peer(i))

    def hz_got(i):
        p = peer(i)
        return copy(chunk(p, g), chunk(p, g), hz_s.at[i], hz_r.at[p], fsdp=p)

    def hx_copy(k):
        p = peer(k)
        return copy(chunk(p, g), chunk(p, g), hx_s.at[k], hx_r.at[k], expert=far)

    def hx_got(k):
        p = peer(k)
        return copy(chunk(p, far), chunk(p, far), hx_s.at[k], hx_r.at[k], expert=far)

    def hc_copy(k, t):
        p = peer(k)
        c = chunk(p, (g, far)[t])
        return copy(c, c, hc_s.at[k, t], hc_r.at[k, t], expert=near)

    def hc_got(k, t):
        p = peer(k)
        c = chunk(p, (near, both)[t])
        return copy(c, c, hc_s.at[k, t], hc_r.at[k, t], expert=near)

    def forward(n):
        hz_got(n).wait_recv()
        hx_copy(n).start()
        hc_copy(n, 0).start()

    hx_copy(0).start()
    hz_copy(1).start()
    hc_copy(0, 0).start()
    inner = lax.rem(lax.div(lax.rem(f, 4) + 1, 2), 2) == 1
    pl.when(inner)(lambda: hz_copy(2).start())
    hz_copy(1).wait_send()
    pl.when(jnp.logical_not(inner))(lambda: hz_copy(2).start())
    forward(1)
    loop(3, F, lambda i: hz_copy(i).start())

    def step(k):
        p = peer(k)
        hx_got(k).wait_recv()
        hc_copy(k, 1).start()
        hc_got(k, 0).wait_recv()
        hc_got(k, 1).wait_recv()
        gain = gain_ref[p]

        def dispatch(s):
            rows = jnp.dot(oh[s, :, :Q].astype(BF16), h_all[p, s], preferred_element_type=F32)
            at = s * CAP if isinstance(s, int) else pl.multiple_of(s * CAP, 8)
            square = jnp.sum(rows * rows, axis=1, keepdims=True)
            rows = rows * gain
            for e in range(2):
                lhs[e, pl.ds(at, CAP), :] = rows[e * CAP:(e + 1) * CAP]
                ssq[e, pl.ds(at, CAP), :] += jnp.broadcast_to(square[e * CAP:(e + 1) * CAP], (CAP, 128))

        loop(0, F, dispatch)
        two = k % 2
        copies = w_copies(k)
        for e in range(2):
            x = lhs[e].astype(BF16)
            for t in range(2):
                copies[2 * e + t].wait()
                y = jnp.dot(x, wslot[two, 2 * e + t], preferred_element_type=F32)
                if isinstance(k, int) and k == 0:
                    acc[e, t] = y
                else:
                    acc[e, t] += y
            if e == 0:
                when(k + 2 < F, lambda: forward(k + 2))

        def refill():
            for c in w_copies(k + 2):
                c.start()

        when(k + 2 < F, refill)

    if F > 8:
        acc[...] = jnp.zeros_like(acc)
    loop(0, F, step)

    for e in range(2):
        scale = lax.rsqrt(ssq[e][:, :1] / D + EPS)
        gate = acc[e, 0] * scale
        up = acc[e, 1] * scale
        hid[e] = (gate / (1.0 + jnp.exp(-gate)) * up).astype(BF16)

    def a_copy(hh, t):
        return copy(cbuf.at[hh, 0], a_in.at[hh, t], a_s.at[hh, t], a_r.at[hh, t], expert=near)

    def b_copy(hh, s):
        return copy(cbuf.at[hh, 1, s], b_in.at[hh, s], b_s.at[hh, s], b_r.at[hh, s], expert=far)

    def c_copy(hh, s):
        return copy(cbuf.at[hh, 2, s], c_in.at[hh, f], c_s.at[hh, s], c_r.at[hh, f], fsdp=s)

    def c_got(hh, p):
        return copy(c_in.at[hh, p], c_in.at[hh, p], c_s.at[hh, p], c_r.at[hh, p], fsdp=p)

    def order(n):
        return peer(F - 1 - n)

    def down(n):
        hh, i = n // 4, n % 4
        copies = d_copies(n)
        for e in range(2):
            copies[e].wait()
            ybuf[e] = jnp.dot(hid[e], dslot[n % D_SLOTS, e], preferred_element_type=F32)
        if n + D_SLOTS < 4 * HALVES:
            for c in d_copies(n + D_SLOTS):
                c.start()
        if i in (1, 3):
            a_copy(hh, i // 2).wait_recv()
        if i == 2:
            a_copy(hh, 0).wait_send()

        def combine(m):
            s = order(m)
            at = pl.multiple_of(s * CAP, 8)
            ys = jnp.concatenate([ybuf[0, pl.ds(at, CAP), :], ybuf[1, pl.ds(at, CAP), :]], axis=0)
            ys = (ys * oh[s, :, Q:Q + 1]).astype(BF16)
            c = lax.dot_general(
                oh[s, :, :Q].astype(BF16), ys, (((0,), (0,)), ((), ())), preferred_element_type=F32)
            if i in (1, 3):
                c = c + a_in[hh, i // 2, s].astype(F32)
            cbuf[hh, (0, 1, 0, 2)[i], s] = c.astype(BF16)
            if i == 1:
                b_copy(hh, s).start()

        loop(0, F, combine)
        if i in (0, 2):
            a_copy(hh, i // 2).start()

    def send_seq(hh, m):
        s = order(m)
        b_copy(hh, s).wait_recv()
        cbuf[hh, 2, s] = (cbuf[hh, 2, s].astype(F32) + b_in[hh, s].astype(F32)).astype(BF16)
        c_copy(hh, s).start()

    for hh in range(HALVES):
        for i in range(4):
            down(4 * hh + i)
            if hh > 0 and i in (0, 1) and F > 2:
                send_seq(hh - 1, i)
        if hh > 0:
            loop(2 if F > 2 else 0, F - 1, lambda m: send_seq(hh - 1, m))
    loop(0, F - 1, lambda m: send_seq(HALVES - 1, m))

    for hh in range(HALVES):
        b_copy(hh, f).wait_recv()
        ybuf[0, 0:Q, :] = cbuf[hh, 2, f].astype(F32) + b_in[hh, f].astype(F32)

        def add_seq(i):
            p = peer(i)
            c_got(hh, p).wait_recv()
            ybuf[0, 0:Q, :] += c_in[hh, p].astype(F32)

        loop(1, F, add_seq)
        width = min(C, CH)
        for i in range(CH // width):
            at = hh * CH + i * width
            state = h_all[g * FG + at // C, f, :, at % C:at % C + width].astype(F32)
            out_ref[:, at:at + width] = (state + ybuf[0, 0:Q, i * width:(i + 1) * width]).astype(BF16)

    def drain(i):
        rt_copy(i).wait_send()
        hs_copy(i).wait_send()
        for hh in range(HALVES):
            c_copy(hh, peer(i)).wait_send()

    loop(1, F, drain)
    loop(2, F, lambda i: hz_copy(i).wait_send())

    @pl.when(own_part)
    def _():
        loop(1, F, lambda i: re_copy(i).wait_send())

    for e in (near, far, both):
        rs_copy(e).wait_send()

    def drain_all(k):
        hx_copy(k).wait_send()
        hc_copy(k, 0).wait_send()
        hc_copy(k, 1).wait_send()
        for hh in range(HALVES):
            b_copy(hh, k).wait_send()

    loop(0, F, drain_all)
    for hh in range(HALVES):
        a_copy(hh, 1).wait_send()


def layer(F, G, queries, keys, values, out_weight, residual, norm_gain,
          route_ids, route_slots, route_weights, w_gate, w_up, w_down):
    Q = queries.shape[0]
    D = residual.shape[1]
    C = out_weight.shape[1]
    H = w_gate.shape[2]
    R = CAP * F
    FG = F // G
    C2 = D // G
    CH = C2 // HALVES
    gain = norm_gain.reshape(F, 1, C)
    vm = pl.BlockSpec(memory_space=pltpu.VMEM)
    hbm = pl.BlockSpec(memory_space=pltpu.HBM)
    dma = pltpu.SemaphoreType.DMA
    return pl.pallas_call(
        functools.partial(kernel, F, G),
        out_shape=jax.ShapeDtypeStruct((Q, C2), BF16),
        in_specs=[hbm] * 5 + [vm] * 4 + [hbm] * 3,
        out_specs=vm,
        scratch_shapes=[
            pltpu.VMEM(queries.shape, BF16),
            pltpu.VMEM(keys.shape[1:], BF16),
            pltpu.VMEM(values.shape[1:], BF16),
            pltpu.VMEM(out_weight.shape, BF16),
            pltpu.VMEM(residual.shape, BF16),
            pltpu.VMEM((F, Q, queries.shape[1]), BF16),
            pltpu.VMEM((F, 8, 128), jnp.int32),
            pltpu.VMEM((FG, Q, C), BF16),
            pltpu.VMEM((G, FG, Q, C), BF16),
            pltpu.VMEM((G, FG, Q, C), BF16),
            pltpu.VMEM((FG, Q, C), F32),
            pltpu.VMEM((F, F, Q, C), BF16),
            pltpu.VMEM((F, 2 * CAP, 128), F32),
            pltpu.VMEM((2, R, C), F32),
            pltpu.VMEM((2, R, 128), F32),
            pltpu.VMEM((2, 2, R, H), F32),
            pltpu.VMEM((2, R, H), BF16),
            pltpu.VMEM((2, R, CH), F32),
            pltpu.VMEM((HALVES, 3, F, Q, CH), BF16),
            pltpu.VMEM((HALVES, 2, F, Q, CH), BF16),
            pltpu.VMEM((HALVES, F, Q, CH), BF16),
            pltpu.VMEM((HALVES, F, Q, CH), BF16),
            pltpu.VMEM((2, 4, C, H), BF16),
            pltpu.VMEM((D_SLOTS, 2, H, CH), BF16),
            dma((5,)), dma((F,)), dma((F,)), dma((F,)), dma((F,)), dma((F,)), dma((FG,)),
            dma((G,)), dma((G,)), dma((F,)), dma((F,)), dma((F,)), dma((F,)),
            dma((F, 2)), dma((F, 2)), dma((HALVES, 2)), dma((HALVES, 2)), dma((HALVES, F)), dma((HALVES, F)),
            dma((HALVES, F)), dma((HALVES, F)), dma((2, 4)), dma((D_SLOTS, 2)),
        ],
        compiler_params=pltpu.CompilerParams(
            collective_id=0, has_side_effects=True, vmem_limit_bytes=67043328),
    )(queries, keys[0], values[0], out_weight, residual, gain,
      route_ids.T, route_slots.T, route_weights.T, w_gate, w_up, w_down)


def solution(mesh):
    F, G = mesh.shape["fsdp"], mesh.shape["expert"]
    rows = P(("groups", "fsdp"), None)
    in_specs = (
        P(("groups", "fsdp"), "expert"),
        P(("groups", "fsdp"), None, "expert"),
        P(("groups", "fsdp"), None, "expert"),
        P("expert", "fsdp"),
        rows, P(), rows, rows, rows,
        P("expert", None, "fsdp"),
        P("expert", None, "fsdp"),
        P("expert", "fsdp", None),
    )
    return jax.shard_map(
        functools.partial(layer, F, G), mesh=mesh, in_specs=in_specs,
        out_specs=P(("groups", "fsdp"), "expert"), check_vma=False,
    )
```

time: 77.8 us -> 71.8 us (0.923)
  Pallas kernels: 74.7 us -> 70 us
    pallas_call x1, Pallas kernels: 74.7 us -> 70 us  [layer(): pl.pallas_call(functools.partial(kernel, F, G), out_shape=jax.ShapeDtypeS...]
where the time goes in v1:
time: 71.8 us; the launch traced here: 71.5 us
  Pallas kernels  70 us (97%)
  local copies, waits for them, and re-layouts  1.57 us (2%)
    pallas_call x1, Pallas kernels, layer(): pl.pallas_call(functools.partial(kernel, F, G), out_shape=jax.ShapeDtypeS...  70 us
    unnamed x1, local copies, waits for them, and re-layouts  1.57 us

profile of v1, /device:TPU:0, one launch (start us, length us, event | category | flops | bytes accessed | tf_op | source)
XLA Modules:
  0.0 71.5 jit_solution(10401814148906079826)
XLA Ops:
  0.0 70.0 %shard_map.118 = bf16[64,1024]{1,0:T(8,128)(2,1)} custom-call(bf16[64,512]{1,0:T(8,128)(2,1)} %q_hbm.1, bf16[2048,128]{1,0:T(8,128)(2,1)} %bitcast.6, bf16[2048,128]{1,0:T(8,128)(2,1)} %bitcast.7, bf16[512,1024]{1,0:T(8,128)(2,1)} %ow_hbm.1, bf16[64,4096]{1,0:T(8,128)(2,1)} %res_hbm.1, f32[4,1,1024]{2,1,0:T(1,128)} %bitcast.8, s32[2,64]{1,0:T(2,128)} %bitcast.9, ...), custom_call_target="tpu_custom_call" | custom-call | tf_op jit(solution)/shard_map/pallas_call | solution.py:472
  70.0 1.6 %copy.14 = bf16[64,1024]{1,0:T(8,128)(2,1)} copy(bf16[64,1024]{1,0:T(8,128)(2,1)} %shard_map.118) | data formatting | bytes 262144

commit v2 on v1

--- a/solution.py
+++ b/solution.py
@@ -15,6 +15,7 @@
 BF16 = jnp.bfloat16
 HALVES = 2
 D_SLOTS = 4
+VMEM = 67043328
 
 
 def loop(low, high, body):
@@ -39,7 +40,7 @@
     out_ref,
     q_ref, k_ref, v_ref, ow_ref, res_ref,
     heads, routes, res_in, part, rs_in, attn_own, h_all, oh, lhs, ssq, acc, hid, ybuf,
-    cbuf, a_in, b_in, c_in, wslot, dslot,
+    abuf, cbuf, a_in, b_in, c_in, wslot, dslot,
     in_sem, hs_s, hs_r, rt_s, rt_r, re_s, re_r, rs_s, rs_r, hz_s, hz_r, hx_s, hx_r, hc_s, hc_r,
     a_s, a_r, b_s, b_r, c_s, c_r, w_sem, d_sem,
 ):
@@ -71,6 +72,23 @@
             bit *= 2
         return out
 
+    def half(a):
+        return a // 2 if isinstance(a, int) else lax.div(a, 2)
+
+    def home(s):
+        quarter = s // FG
+        high = half(quarter)
+        low = quarter - 2 * high
+        return 2 * (low + high - 2 * low * high) + high
+
+    def first_seq(e):
+        high = half(e)
+        low = e - 2 * high
+        return (2 * low + high + low - 2 * high * low) * FG
+
+    def slot(s):
+        return home(s) * FG + s % FG
+
     def peer(i):
         if F & (F - 1) == 0:
             return flip(f, i, F)
@@ -111,7 +129,7 @@
                     ref.at[e, rows, :], wslot.at[two, 2 * e + t], w_sem.at[two, 2 * e + t]))
         return out
 
-    masks = (3, 2, 1, 0)
+    masks = (3, 1, 2, 0)
 
     def d_copies(n):
         block = flip(g, masks[n % 4], G)
@@ -167,7 +185,7 @@
     def cols_of(p):
         return pl.ds(pl.multiple_of(p * C, C), C)
 
-    own_part = (f // FG) == g
+    own_part = home(f) == g
     mine = f % FG
 
     def re_copy(i):
@@ -183,9 +201,8 @@
     loop(1, F, lambda i: hs_copy(i).start())
     loop(1, F, lambda i: rt_copy(i).start())
 
-    @pl.when(own_part)
-    def _():
-        loop(1, F, lambda i: re_copy(i).start())
+    def send_res():
+        loop(1, F, lambda i: re_copy(F - i).start())
         res_in[mine] = res_ref[:, cols_of(f)]
 
     ssq[...] = jnp.zeros_like(ssq)
@@ -197,17 +214,18 @@
         return copy(part.at[e], rs_in.at[e], rs_s.at[e], rs_r.at[e], expert=e)
 
     def project(i):
-        j = flip(f // FG, i, G)
+        base = flip(f // FG, i, G) * FG
+        j = home(base)
 
         def arrive(n):
-            p = j * FG + n
+            p = base + n
 
             @pl.when(p != f)
             def _():
                 hs_got(p).wait_recv()
 
         loop(0, FG, arrive)
-        rows = heads[pl.ds(j * FG, FG)].reshape(FG * Q, n_heads * HEAD_DIM)
+        rows = heads[pl.ds(base, FG)].reshape(FG * Q, n_heads * HEAD_DIM)
         y = jnp.dot(rows, ow_ref[...], preferred_element_type=F32).reshape(FG, Q, C)
 
         @pl.when(j == g)
@@ -221,6 +239,8 @@
 
     for i in range(G):
         project(i)
+        if i == 1:
+            pl.when(own_part)(send_res)
 
     loop(1, F, lambda i: rt_got(i).wait_recv())
 
@@ -244,11 +264,11 @@
     far, near, both = flip(g, 2, G), flip(g, 1, G), flip(g, 3, G)
 
     def re_got(i):
-        p = g * FG + i
+        p = first_seq(g) + i
         return copy(res_in.at[i], res_in.at[i], re_s.at[0], re_r.at[i], fsdp=p)
 
     def take_res(i):
-        @pl.when(g * FG + i != f)
+        @pl.when(first_seq(g) + i != f)
         def _():
             re_got(i).wait_recv()
 
@@ -311,7 +331,7 @@
         gain = gain_ref[p]
 
         def dispatch(s):
-            rows = jnp.dot(oh[s, :, :Q].astype(BF16), h_all[p, s], preferred_element_type=F32)
+            rows = jnp.dot(oh[s, :, :Q].astype(BF16), h_all[p, slot(s)], preferred_element_type=F32)
             at = s * CAP if isinstance(s, int) else pl.multiple_of(s * CAP, 8)
             square = jnp.sum(rows * rows, axis=1, keepdims=True)
             rows = rows * gain
@@ -321,11 +341,11 @@
 
         loop(0, F, dispatch)
         two = k % 2
-        copies = w_copies(k)
+        for c in w_copies(k):
+            c.wait()
         for e in range(2):
             x = lhs[e].astype(BF16)
             for t in range(2):
-                copies[2 * e + t].wait()
                 y = jnp.dot(x, wslot[two, 2 * e + t], preferred_element_type=F32)
                 if isinstance(k, int) and k == 0:
                     acc[e, t] = y
@@ -351,13 +371,13 @@
         hid[e] = (gate / (1.0 + jnp.exp(-gate)) * up).astype(BF16)
 
     def a_copy(hh, t):
-        return copy(cbuf.at[hh, 0], a_in.at[hh, t], a_s.at[hh, t], a_r.at[hh, t], expert=near)
+        return copy(abuf.at[t], a_in.at[hh, t], a_s.at[hh, t], a_r.at[hh, t], expert=near)
 
     def b_copy(hh, s):
-        return copy(cbuf.at[hh, 1, s], b_in.at[hh, s], b_s.at[hh, s], b_r.at[hh, s], expert=far)
+        return copy(cbuf.at[hh, 0, s], b_in.at[hh, s], b_s.at[hh, s], b_r.at[hh, s], expert=far)
 
     def c_copy(hh, s):
-        return copy(cbuf.at[hh, 2, s], c_in.at[hh, f], c_s.at[hh, s], c_r.at[hh, f], fsdp=s)
+        return copy(cbuf.at[hh, 1, s], c_in.at[hh, f], c_s.at[hh, s], c_r.at[hh, f], fsdp=s)
 
     def c_got(hh, p):
         return copy(c_in.at[hh, p], c_in.at[hh, p], c_s.at[hh, p], c_r.at[hh, p], fsdp=p)
@@ -367,17 +387,15 @@
 
     def down(n):
         hh, i = n // 4, n % 4
-        copies = d_copies(n)
+        for c in d_copies(n):
+            c.wait()
         for e in range(2):
-            copies[e].wait()
             ybuf[e] = jnp.dot(hid[e], dslot[n % D_SLOTS, e], preferred_element_type=F32)
         if n + D_SLOTS < 4 * HALVES:
             for c in d_copies(n + D_SLOTS):
                 c.start()
-        if i in (1, 3):
-            a_copy(hh, i // 2).wait_recv()
-        if i == 2:
-            a_copy(hh, 0).wait_send()
+        if i in (2, 3):
+            a_copy(hh, i - 2).wait_recv()
 
         def combine(m):
             s = order(m)
@@ -386,34 +404,37 @@
             ys = (ys * oh[s, :, Q:Q + 1]).astype(BF16)
             c = lax.dot_general(
                 oh[s, :, :Q].astype(BF16), ys, (((0,), (0,)), ((), ())), preferred_element_type=F32)
-            if i in (1, 3):
-                c = c + a_in[hh, i // 2, s].astype(F32)
-            cbuf[hh, (0, 1, 0, 2)[i], s] = c.astype(BF16)
-            if i == 1:
-                b_copy(hh, s).start()
-
+            if i in (2, 3):
+                c = c + a_in[hh, i - 2, s].astype(F32)
+            if i < 2:
+                abuf[i, s] = c.astype(BF16)
+            else:
+                cbuf[hh, i - 2, s] = c.astype(BF16)
+
+        if i < 2 and hh > 0:
+            a_copy(hh - 1, i).wait_send()
         loop(0, F, combine)
-        if i in (0, 2):
-            a_copy(hh, i // 2).start()
+        if i < 2:
+            a_copy(hh, i).start()
+        if i == 2:
+            loop(0, F, lambda m: b_copy(hh, order(m)).start())
 
     def send_seq(hh, m):
         s = order(m)
         b_copy(hh, s).wait_recv()
-        cbuf[hh, 2, s] = (cbuf[hh, 2, s].astype(F32) + b_in[hh, s].astype(F32)).astype(BF16)
+        cbuf[hh, 1, s] = (cbuf[hh, 1, s].astype(F32) + b_in[hh, s].astype(F32)).astype(BF16)
         c_copy(hh, s).start()
 
     for hh in range(HALVES):
         for i in range(4):
             down(4 * hh + i)
-            if hh > 0 and i in (0, 1) and F > 2:
-                send_seq(hh - 1, i)
-        if hh > 0:
-            loop(2 if F > 2 else 0, F - 1, lambda m: send_seq(hh - 1, m))
+            if hh > 0:
+                loop((F - 1) * i // 4, (F - 1) * (i + 1) // 4, lambda m: send_seq(hh - 1, m))
     loop(0, F - 1, lambda m: send_seq(HALVES - 1, m))
 
     for hh in range(HALVES):
         b_copy(hh, f).wait_recv()
-        ybuf[0, 0:Q, :] = cbuf[hh, 2, f].astype(F32) + b_in[hh, f].astype(F32)
+        ybuf[0, 0:Q, :] = cbuf[hh, 1, f].astype(F32) + b_in[hh, f].astype(F32)
 
         def add_seq(i):
             p = peer(i)
@@ -424,7 +445,7 @@
         width = min(C, CH)
         for i in range(CH // width):
             at = hh * CH + i * width
-            state = h_all[g * FG + at // C, f, :, at % C:at % C + width].astype(F32)
+            state = h_all[g * FG + at // C, slot(f), :, at % C:at % C + width].astype(F32)
             out_ref[:, at:at + width] = (state + ybuf[0, 0:Q, i * width:(i + 1) * width]).astype(BF16)
 
     def drain(i):
@@ -451,8 +472,8 @@
             b_copy(hh, k).wait_send()
 
     loop(0, F, drain_all)
-    for hh in range(HALVES):
-        a_copy(hh, 1).wait_send()
+    for t in range(2):
+        a_copy(HALVES - 1, t).wait_send()
 
 
 def layer(F, G, queries, keys, values, out_weight, residual, norm_gain,
@@ -493,7 +514,8 @@
             pltpu.VMEM((2, 2, R, H), F32),
             pltpu.VMEM((2, R, H), BF16),
             pltpu.VMEM((2, R, CH), F32),
-            pltpu.VMEM((HALVES, 3, F, Q, CH), BF16),
+            pltpu.VMEM((2, F, Q, CH), BF16),
+            pltpu.VMEM((HALVES, 2, F, Q, CH), BF16),
             pltpu.VMEM((HALVES, 2, F, Q, CH), BF16),
             pltpu.VMEM((HALVES, F, Q, CH), BF16),
             pltpu.VMEM((HALVES, F, Q, CH), BF16),
@@ -505,7 +527,7 @@
             dma((HALVES, F)), dma((HALVES, F)), dma((2, 4)), dma((D_SLOTS, 2)),
         ],
         compiler_params=pltpu.CompilerParams(
-            collective_id=0, has_side_effects=True, vmem_limit_bytes=67043328),
+            collective_id=0, has_side_effects=True, vmem_limit_bytes=VMEM),
     )(queries, keys[0], values[0], out_weight, residual, gain,
       route_ids.T, route_slots.T, route_weights.T, w_gate, w_up, w_down)
 

time: 71.8 us -> 64.7 us (0.901)
  Pallas kernels: 70 us -> 62.9 us
    pallas_call x1, Pallas kernels: 70 us -> 62.9 us  [layer(): pl.pallas_call(functools.partial(kernel, F, G), out_shape=jax.ShapeDtypeS...]
where the time goes in v2:
time: 64.7 us; the launch traced here: 64.4 us
  Pallas kernels  62.9 us (97%)
  local copies, waits for them, and re-layouts  1.57 us (2%)
    pallas_call x1, Pallas kernels, layer(): pl.pallas_call(functools.partial(kernel, F, G), out_shape=jax.ShapeDtypeS...  62.9 us
    unnamed x1, local copies, waits for them, and re-layouts  1.57 us

profile of v2, /device:TPU:0, one launch (start us, length us, event | category | flops | bytes accessed | tf_op | source)
XLA Modules:
  0.0 64.4 jit_solution(9210174807557901469)
XLA Ops:
  0.0 62.9 %shard_map.118 = bf16[64,1024]{1,0:T(8,128)(2,1)} custom-call(bf16[64,512]{1,0:T(8,128)(2,1)} %q_hbm.1, bf16[2048,128]{1,0:T(8,128)(2,1)} %bitcast.6, bf16[2048,128]{1,0:T(8,128)(2,1)} %bitcast.7, bf16[512,1024]{1,0:T(8,128)(2,1)} %ow_hbm.1, bf16[64,4096]{1,0:T(8,128)(2,1)} %res_hbm.1, f32[4,1,1024]{2,1,0:T(1,128)} %bitcast.8, s32[2,64]{1,0:T(2,128)} %bitcast.9, ...), custom_call_target="tpu_custom_call" | custom-call | tf_op jit(solution)/shard_map/pallas_call | solution.py:493
  62.9 1.6 %copy.14 = bf16[64,1024]{1,0:T(8,128)(2,1)} copy(bf16[64,1024]{1,0:T(8,128)(2,1)} %shard_map.118) | data formatting | bytes 262144

commit v3 on v2

--- a/solution.py
+++ b/solution.py
@@ -202,7 +202,7 @@
     loop(1, F, lambda i: rt_copy(i).start())
 
     def send_res():
-        loop(1, F, lambda i: re_copy(F - i).start())
+        loop(1, F, lambda i: re_copy(i).start())
         res_in[mine] = res_ref[:, cols_of(f)]
 
     ssq[...] = jnp.zeros_like(ssq)
@@ -282,20 +282,26 @@
     def chunk(p, e):
         return h_all.at[p, pl.ds(e * FG, FG)]
 
-    def hz_copy(i):
-        return copy(chunk(f, g), chunk(f, g), hz_s.at[i], hz_r.at[f], fsdp=peer(i))
-
-    def hz_got(i):
+    pieces = 2 if C % 256 == 0 else 1
+    CP = C // pieces
+
+    def piece(p, e, t):
+        return h_all.at[p, pl.ds(e * FG, FG), :, pl.ds(t * CP, CP)]
+
+    def hz_copy(i, t):
+        return copy(piece(f, g, t), piece(f, g, t), hz_s.at[i, t], hz_r.at[f, t], fsdp=peer(i))
+
+    def hz_got(i, t):
         p = peer(i)
-        return copy(chunk(p, g), chunk(p, g), hz_s.at[i], hz_r.at[p], fsdp=p)
-
-    def hx_copy(k):
+        return copy(piece(p, g, t), piece(p, g, t), hz_s.at[i, t], hz_r.at[p, t], fsdp=p)
+
+    def hx_copy(k, t):
         p = peer(k)
-        return copy(chunk(p, g), chunk(p, g), hx_s.at[k], hx_r.at[k], expert=far)
-
-    def hx_got(k):
+        return copy(piece(p, g, t), piece(p, g, t), hx_s.at[k, t], hx_r.at[k, t], expert=far)
+
+    def hx_got(k, t):
         p = peer(k)
-        return copy(chunk(p, far), chunk(p, far), hx_s.at[k], hx_r.at[k], expert=far)
+        return copy(piece(p, far, t), piece(p, far, t), hx_s.at[k, t], hx_r.at[k, t], expert=far)
 
     def hc_copy(k, t):
         p = peer(k)
@@ -308,23 +314,32 @@
         return copy(c, c, hc_s.at[k, t], hc_r.at[k, t], expert=near)
 
     def forward(n):
-        hz_got(n).wait_recv()
-        hx_copy(n).start()
+        for t in range(pieces):
+            hz_got(n, t).wait_recv()
+            hx_copy(n, t).start()
         hc_copy(n, 0).start()
 
-    hx_copy(0).start()
-    hz_copy(1).start()
+    def spread(i):
+        for t in range(pieces):
+            hz_copy(i, t).start()
+
+    for t in range(pieces):
+        hx_copy(0, t).start()
+    spread(1)
     hc_copy(0, 0).start()
-    inner = lax.rem(lax.div(lax.rem(f, 4) + 1, 2), 2) == 1
-    pl.when(inner)(lambda: hz_copy(2).start())
-    hz_copy(1).wait_send()
-    pl.when(jnp.logical_not(inner))(lambda: hz_copy(2).start())
+    loop(2, F, spread)
     forward(1)
-    loop(3, F, lambda i: hz_copy(i).start())
+
+    def act(e):
+        scale = lax.rsqrt(ssq[e][:, :1] / D + EPS)
+        gate = acc[e, 0] * scale
+        up = acc[e, 1] * scale
+        hid[e] = (gate / (1.0 + jnp.exp(-gate)) * up).astype(BF16)
 
     def step(k):
         p = peer(k)
-        hx_got(k).wait_recv()
+        for t in range(pieces):
+            hx_got(k, t).wait_recv()
         hc_copy(k, 1).start()
         hc_got(k, 0).wait_recv()
         hc_got(k, 1).wait_recv()
@@ -351,6 +366,8 @@
                     acc[e, t] = y
                 else:
                     acc[e, t] += y
+            if isinstance(k, int) and k == F - 1:
+                act(e)
             if e == 0:
                 when(k + 2 < F, lambda: forward(k + 2))
 
@@ -362,13 +379,13 @@
 
     if F > 8:
         acc[...] = jnp.zeros_like(acc)
+    for c in d_copies(0):
+        c.wait()
     loop(0, F, step)
 
-    for e in range(2):
-        scale = lax.rsqrt(ssq[e][:, :1] / D + EPS)
-        gate = acc[e, 0] * scale
-        up = acc[e, 1] * scale
-        hid[e] = (gate / (1.0 + jnp.exp(-gate)) * up).astype(BF16)
+    if F > 8:
+        for e in range(2):
+            act(e)
 
     def a_copy(hh, t):
         return copy(abuf.at[t], a_in.at[hh, t], a_s.at[hh, t], a_r.at[hh, t], expert=near)
@@ -387,8 +404,9 @@
 
     def down(n):
         hh, i = n // 4, n % 4
-        for c in d_copies(n):
-            c.wait()
+        if n > 0:
+            for c in d_copies(n):
+                c.wait()
         for e in range(2):
             ybuf[e] = jnp.dot(hid[e], dslot[n % D_SLOTS, e], preferred_element_type=F32)
         if n + D_SLOTS < 4 * HALVES:
@@ -455,7 +473,12 @@
             c_copy(hh, peer(i)).wait_send()
 
     loop(1, F, drain)
-    loop(2, F, lambda i: hz_copy(i).wait_send())
+
+    def drain_h(i):
+        for t in range(pieces):
+            hz_copy(i, t).wait_send()
+
+    loop(1, F, drain_h)
 
     @pl.when(own_part)
     def _():
@@ -465,7 +488,8 @@
         rs_copy(e).wait_send()
 
     def drain_all(k):
-        hx_copy(k).wait_send()
+        for t in range(pieces):
+            hx_copy(k, t).wait_send()
         hc_copy(k, 0).wait_send()
         hc_copy(k, 1).wait_send()
         for hh in range(HALVES):
@@ -522,7 +546,7 @@
             pltpu.VMEM((2, 4, C, H), BF16),
             pltpu.VMEM((D_SLOTS, 2, H, CH), BF16),
             dma((5,)), dma((F,)), dma((F,)), dma((F,)), dma((F,)), dma((F,)), dma((FG,)),
-            dma((G,)), dma((G,)), dma((F,)), dma((F,)), dma((F,)), dma((F,)),
+            dma((G,)), dma((G,)), dma((F, 2)), dma((F, 2)), dma((F, 2)), dma((F, 2)),
             dma((F, 2)), dma((F, 2)), dma((HALVES, 2)), dma((HALVES, 2)), dma((HALVES, F)), dma((HALVES, F)),
             dma((HALVES, F)), dma((HALVES, F)), dma((2, 4)), dma((D_SLOTS, 2)),
         ],

time: 64.7 us -> 64 us (0.989)
  Pallas kernels: 62.9 us -> 62.2 us
where the time goes in v3:
time: 64 us; the launch traced here: 63.8 us
  Pallas kernels  62.2 us (97%)
  local copies, waits for them, and re-layouts  1.57 us (2%)
    pallas_call x1, Pallas kernels, layer(): pl.pallas_call(functools.partial(kernel, F, G), out_shape=jax.ShapeDtypeS...  62.2 us
    unnamed x1, local copies, waits for them, and re-layouts  1.57 us

profile of v3, /device:TPU:0, one launch (start us, length us, event | category | flops | bytes accessed | tf_op | source)
XLA Modules:
  0.0 63.8 jit_solution(9959085460779696432)
XLA Ops:
  0.0 62.2 %shard_map.118 = bf16[64,1024]{1,0:T(8,128)(2,1)} custom-call(bf16[64,512]{1,0:T(8,128)(2,1)} %q_hbm.1, bf16[2048,128]{1,0:T(8,128)(2,1)} %bitcast.6, bf16[2048,128]{1,0:T(8,128)(2,1)} %bitcast.7, bf16[512,1024]{1,0:T(8,128)(2,1)} %ow_hbm.1, bf16[64,4096]{1,0:T(8,128)(2,1)} %res_hbm.1, f32[4,1,1024]{2,1,0:T(1,128)} %bitcast.8, s32[2,64]{1,0:T(2,128)} %bitcast.9, ...), custom_call_target="tpu_custom_call" | custom-call | tf_op jit(solution)/shard_map/pallas_call | solution.py:517
  62.2 1.6 %copy.14 = bf16[64,1024]{1,0:T(8,128)(2,1)} copy(bf16[64,1024]{1,0:T(8,128)(2,1)} %shard_map.118) | data formatting | bytes 262144
